TPU v7x, 32 devices: a whole 2x2x4 slice. The times are simulated.
32 devices in a mesh: head: 8 (over z, core), kv: 4 (over y, x).
Axes of the slice: x: 2, y: 2, z: 4, core: 2. Of those that a mesh axis runs over, the one named last changes fastest.
Arguments:
- queries: bfloat16 [2048, 8192], P(('kv', 'head')), may hold values from -6 to 6
- key_rows: bfloat16 [2048, 1024], P(('kv', 'head')), may hold values from -6 to 6
- value_matrix: bfloat16 [2048, 1024], P(('kv', 'head')), may hold values from -6 to 6
- doc_ids: int32 [2048], P(('kv', 'head')), may hold values from 0 to 5, as said below
Outputs:
- attended: bfloat16 [2048, 8192], P(('kv', 'head'))
Inputs may be any that keep to these rules, and one draw needn't show every extreme that they name: doc_ids starts at 0, never falls, and rises by one at the first token of each of the 6 documents; every document starts at an even position and has 2 tokens or more.
All inputs are finite; a program needn't handle non-finite values.
Results may differ from a plain program's by a relative error of at most 0.015.
Values may be sent and summed in bfloat16 or wider, within the bound.
A program may use at most 64 MiB of HBM per device.

v0:
```python
import math

import jax
import jax.numpy as jnp
from jax import lax
from jax.sharding import PartitionSpec as P

QUERY_HEADS = 64
KEY_VALUE_HEADS = 8
HEAD_SIZE = 128


NEG_FILL = -1e30


def repeat_heads(input_matrix, head_repeats):
    row_number = input_matrix.shape[0]
    heads_apart = input_matrix.reshape(row_number, KEY_VALUE_HEADS, 1, HEAD_SIZE)
    expanded_heads = jnp.broadcast_to(
        heads_apart, (row_number, KEY_VALUE_HEADS, head_repeats, HEAD_SIZE)
    )
    return expanded_heads.reshape(row_number, KEY_VALUE_HEADS * head_repeats * HEAD_SIZE)


def block_terms(query_group, query_pos, query_doc, key_block, value_block, key_pos, key_doc):
    key_count = key_block.shape[0]
    key_value_slot = query_group.shape[1]
    key_heads = key_block.reshape(key_count, key_value_slot, HEAD_SIZE)
    value_heads = value_block.reshape(key_count, key_value_slot, HEAD_SIZE)
    scores = jnp.einsum(
        "rkgd,ckd->kgrc", query_group, key_heads, preferred_element_type=jnp.float32
    ) * HEAD_SIZE ** (-0.5)
    allowed = (key_pos[None, :] <= query_pos[:, None]) & (key_doc[None, :] == query_doc[:, None])
    masked = jnp.where(allowed, scores, NEG_FILL)
    row_peak = jnp.max(masked, axis=-1)
    weights = jnp.where(allowed, jnp.exp(masked - row_peak[..., None]), 0.0)
    row_total = jnp.sum(weights, axis=-1)
    weighted = jnp.einsum(
        "kgrc,ckd->kgrd",
        weights.astype(jnp.bfloat16),
        value_heads,
        preferred_element_type=jnp.float32,
    )
    return (row_peak, row_total, weighted)


def attend_block(query_group, query_pos, query_doc, key_block, value_block, key_pos, key_doc):
    return block_terms(query_group, query_pos, query_doc, key_block, value_block, key_pos, key_doc)


def combine_terms(first_terms, second_terms):
    joint_peak = jnp.maximum(first_terms[0], second_terms[0])
    left_factor = jnp.exp(first_terms[0] - joint_peak)
    right_factor = jnp.exp(second_terms[0] - joint_peak)
    joint_total = first_terms[1] * left_factor + second_terms[1] * right_factor
    joint_weighted = (
        first_terms[2] * left_factor[..., None] + second_terms[2] * right_factor[..., None]
    )
    return (joint_peak, joint_total, joint_weighted)


def local(queries, key_rows, value_matrix, doc_ids):
    head_number = lax.axis_size("head")
    head_repeats = max(1, head_number // KEY_VALUE_HEADS)
    key_send = repeat_heads(key_rows, head_repeats)
    value_send = repeat_heads(value_matrix, head_repeats)
    query_block, key_block, value_block = (
        lax.all_to_all(queries, "head", split_axis=1, concat_axis=0, tiled=True),
        lax.all_to_all(key_send, "head", split_axis=1, concat_axis=0, tiled=True),
        lax.all_to_all(value_send, "head", split_axis=1, concat_axis=0, tiled=True),
    )
    block_len = query_block.shape[0]
    doc_global = lax.all_gather(doc_ids, ("kv", "head"), axis=0, tiled=True)
    query_width = query_block.shape[1]
    present_heads = query_width // HEAD_SIZE
    key_value_slot = max(1, present_heads // (QUERY_HEADS // KEY_VALUE_HEADS))
    group_here = present_heads // key_value_slot
    own_first = lax.axis_index("kv") * block_len
    own_pos = own_first + jnp.arange(block_len, dtype=jnp.int32)
    own_doc = jnp.take(doc_global, own_pos)
    query_group = query_block.reshape(block_len, key_value_slot, group_here, HEAD_SIZE)
    term_shape = (key_value_slot, group_here, block_len)
    initial = (
        jnp.full(term_shape, NEG_FILL, jnp.float32),
        jnp.zeros(term_shape, jnp.float32),
        jnp.zeros(term_shape + (HEAD_SIZE,), jnp.float32),
    )
    key_piece = lax.all_gather(key_block, "kv", axis=0, tiled=True)
    value_piece = lax.all_gather(value_block, "kv", axis=0, tiled=True)
    piece_rows = key_piece.shape[0]
    step_rows = math.gcd(piece_rows, 1024)

    def one_step(step_index, inner):
        local_first = step_index * step_rows
        keys_now = lax.dynamic_slice_in_dim(key_piece, local_first, step_rows, 0)
        values_now = lax.dynamic_slice_in_dim(value_piece, local_first, step_rows, 0)
        key_pos = local_first + jnp.arange(step_rows, dtype=jnp.int32)
        key_doc = jnp.take(doc_global, key_pos)
        return combine_terms(
            inner,
            attend_block(query_group, own_pos, own_doc, keys_now, values_now, key_pos, key_doc),
        )

    folded = lax.fori_loop(0, piece_rows // step_rows, one_step, initial)
    result = (
        (folded[2] / folded[1][..., None]).transpose(2, 0, 1, 3).reshape(block_len, query_width)
    )
    result = result.astype(jnp.bfloat16)
    return lax.all_to_all(result, "head", split_axis=0, concat_axis=1, tiled=True)


def solution(mesh):
    return jax.shard_map(
        local,
        mesh=mesh,
        in_specs=(
            P(("kv", "head"), None),
            P(("kv", "head"), None),
            P(("kv", "head"), None),
            P(("kv", "head")),
        ),
        out_specs=P(("kv", "head"), None),
        check_vma=False,
    )
```

profile of v0, /device:TPU:0, one launch (start us, length us, event | category | flops | bytes accessed | tf_op | source)
XLA Modules:
  0.0 176.7 jit_solution(10033229204570758715)
XLA Ops:
  0.0 0.9 copy-done
  0.9 0.7 copy_bitcast_fusion.2
  1.6 6.4 %all-to-all-start = ((bf16[64,8,128]{2,0,1:T(8,128)(2,1)}), bf16[64,8,128]{2,0,1:T(8,128)(2,1)S(1)}, u32[]{:S(2)}, u32[]{:S(2)}) async-start(bf16[64,8,128]{2,0,1:T(8,128)(2,1)} %copy_bitcast_fusion.2), calls=%async_computation | async-start | bytes 262144 | tf_op jit(solution)/shard_map/all_to_all | solution.py:69
  7.9 1.6 copy_bitcast_fusion.1
  9.5 5.2 %all-to-all-done = bf16[64,8,128]{2,0,1:T(8,128)(2,1)S(1)} async-done(((bf16[64,8,128]{2,0,1:T(8,128)(2,1)}), bf16[64,8,128]{2,0,1:T(8,128)(2,1)S(1)}, u32[]{:S(2)}, u32[]{:S(2)}) %all-to-all-start) | async-done | bytes 131104 | tf_op jit(solution)/shard_map/all_to_all | solution.py:69
  14.7 3.4 %all-to-all-start.2 = ((bf16[64,8,128]{2,0,1:T(8,128)(2,1)}), bf16[64,8,128]{2,0,1:T(8,128)(2,1)S(1)}, u32[]{:S(2)}, u32[]{:S(2)}) async-start(bf16[64,8,128]{2,0,1:T(8,128)(2,1)} %copy_bitcast_fusion.1), calls=%async_computation.2 | async-start | bytes 262144 | tf_op jit(solution)/shard_map/all_to_all | solution.py:70
  18.1 2.3 %copy.30 = bf16[8,8,8,1024]{3,2,0,1:T(8,128)(2,1)} copy(bf16[8,8,8,1024]{3,2,1,0:T(8,128)(2,1)} %bitcast.121) | data formatting | bytes 2097152 | tf_op jit(solution)/shard_map/all_to_all | solution.py:68
  20.4 4.4 %all-to-all-done.2 = bf16[64,8,128]{2,0,1:T(8,128)(2,1)S(1)} async-done(((bf16[64,8,128]{2,0,1:T(8,128)(2,1)}), bf16[64,8,128]{2,0,1:T(8,128)(2,1)S(1)}, u32[]{:S(2)}, u32[]{:S(2)}) %all-to-all-start.2) | async-done | bytes 131104 | tf_op jit(solution)/shard_map/all_to_all | solution.py:70
  24.8 3.6 %all-to-all-start.1 = ((bf16[64,8,1024]{2,0,1:T(8,128)(2,1)}), bf16[64,8,1024]{2,0,1:T(8,128)(2,1)S(1)}, u32[]{:S(2)}, u32[]{:S(2)}) async-start(bf16[64,8,1024]{2,0,1:T(8,128)(2,1)} %bitcast.93), calls=%async_computation.1 | async-start | bytes 2097152 | tf_op jit(solution)/shard_map/all_to_all | solution.py:68
  28.4 1.3 dynamic-slice
  30.4 0.9 dynamic-update-slice
  31.2 43.9 %all-reduce = s32[2048]{0:T(1024)S(1)} all-reduce(s32[2048]{0:T(1024)S(1)} %dynamic-update-slice), channel_id=1, replica_groups=mesh['head'=8,'kv'=4] {'kv','head'}, use_global_device_ids=true, to_apply=%add | all-reduce | flops 2048 | bytes 16384
  75.2 3.1 %gather_fusion.1 = s32[512]{0:T(512)S(1)} fusion(s32[2048]{0:T(1024)S(1)} %all-reduce, s32[1024]{0:T(1024)S(1)} %pad_clamp_fusion), kind=kCustom, calls=%fused_computation.1 | custom fusion | bytes 6144 | tf_op jit(solution)/shard_map/jit(_take)/gather | solution.py:80
  78.3 11.6 %all_gather.11 = bf16[2048,128]{1,0:T(8,128)(2,1)S(1)} all-gather(bf16[512,128]{1,0:T(8,128)(2,1)S(1)} %bitcast.124), channel_id=1, replica_groups=mesh['head'=8,'kv'=4] {'kv'}, dimensions={0}, use_global_device_ids=true | all-gather | bytes 655360 | tf_op jit(solution)/shard_map/all_gather | solution.py:89
  89.9 9.0 %all_gather.10 = bf16[2048,128]{1,0:T(8,128)(2,1)S(1)} all-gather(bf16[512,128]{1,0:T(8,128)(2,1)S(1)} %bitcast.123), channel_id=1, replica_groups=mesh['head'=8,'kv'=4] {'kv'}, dimensions={0}, use_global_device_ids=true | all-gather | bytes 655360 | tf_op jit(solution)/shard_map/all_gather | solution.py:88
  99.3 43.2 %while.18 = (s32[]{:T(128)}, f32[1,8,512]{2,1,0:T(8,128)S(1)}, f32[1,8,512]{2,1,0:T(8,128)S(1)}, f32[1,8,512,128]{3,2,1,0:T(8,128)}, s32[2048]{0:T(1024)S(1)}, /...) while((s32[]{:T(128)}, f32[1,8,512]{2,1,0:T(8,128)S(1)}, ...), condition=%wide.region_3.4_spmd.clone, body=%wide.region_0.3_spmd.clone.sunk | while | flops 2205726208 | bytes 75335952 | solution.py:104
  99.4 6.2 %gather_fusion = s32[1024]{0:T(1024)S(1)} fusion(s32[2048]{0:T(1024)S(1)} %get-tuple-element.370, s32[1024]{0:T(1024)S(1)} %broadcast_clamp_fusion.2), kind=kCustom, calls=%fused_computation.clone.clone.1 | custom fusion | bytes 12288 | tf_op jit(solution)/shard_map/while/body/eval_jaxpr/jit(_take)/gather | solution.py:98
  105.6 0.8 compare_and_fusion.2
  106.4 2.9 %fusion.41 = (f32[8,512]{1,0:T(8,128)S(1)}, f32[1024,512,8]{1,0,2:T(8,128)S(1)}) fusion(pred[512,1024]{0,1:T(8,128)(4,1)S(1)} %compare_and_fusion.2, bf16[512,1,8,128]{3,0,2,1:T(8,128)(2,1)S(1)} %get-tuple-element.373, bf16[2048,128]{1,0:T(8,128)(2,1)S(1)} %get-tuple-element.372, s32[]{:T(128)S(6)} %select_n.145), kind=kOutput, calls=%fused_computation.5.clone.1 | convolution fusion | flops 1086320640 | bytes 18628612 | tf_op jit(solution)/shard_map/while/body/eval_jaxpr/rkgd,ckd->kgrc/dot_general | solution.py:30
  109.3 4.0 %fusion.43 = f32[8,512]{1,0:T(8,128)S(1)} fusion(f32[1024,512,8]{1,0,2:T(8,128)S(1)} %get-tuple-element.334, f32[8,512]{1,0:T(8,128)S(1)} %get-tuple-element.332, pred[512,1024]{0,1:T(8,128)(4,1)S(1)} %compare_and_fusion.2), kind=kLoop, calls=%fused_computation.7.clone.1 | loop fusion | flops 20967424 | bytes 17334272 | tf_op jit(solution)/shard_map/while/body/eval_jaxpr/reduce_sum | solution.py:37
  113.4 6.1 %bitcast_add_fusion.2 = f32[1,8,512,128]{3,2,1,0:T(8,128)S(1)} fusion(f32[1,8,512,128]{3,2,1,0:T(8,128)S(1)} %copy-done.1, f32[1024,512,8]{1,0,2:T(8,128)S(1)} %get-tuple-element.334, f32[8,512]{1,0:T(8,128)S(1)} %get-tuple-element.332, pred[512,1024]{0,1:T(8,128)(4,1)S(1)} %compare_and_fusion.2, f32[8,512]{1,0:T(8,128)S(1)} %get-tuple-element.336, ...), kind=kOutput, calls=%fused_computation.11.clone.1 | convolution fusion | flops 1096810496 | bytes 21807108 | tf_op jit(solution)/shard_map/while/body/eval_jaxpr/kgrc,ckd->kgrd/dot_general | solution.py:38
  119.6 1.3 copy-done.2
  120.9 6.2 %gather_fusion = s32[1024]{0:T(1024)S(1)} fusion(s32[2048]{0:T(1024)S(1)} %get-tuple-element.370, s32[1024]{0:T(1024)S(1)} %broadcast_clamp_fusion.2), kind=kCustom, calls=%fused_computation.clone.clone.1 | custom fusion | bytes 12288 | tf_op jit(solution)/shard_map/while/body/eval_jaxpr/jit(_take)/gather | solution.py:98
  127.1 0.8 compare_and_fusion.2
  128.0 2.9 %fusion.41 = (f32[8,512]{1,0:T(8,128)S(1)}, f32[1024,512,8]{1,0,2:T(8,128)S(1)}) fusion(pred[512,1024]{0,1:T(8,128)(4,1)S(1)} %compare_and_fusion.2, bf16[512,1,8,128]{3,0,2,1:T(8,128)(2,1)S(1)} %get-tuple-element.373, bf16[2048,128]{1,0:T(8,128)(2,1)S(1)} %get-tuple-element.372, s32[]{:T(128)S(6)} %select_n.145), kind=kOutput, calls=%fused_computation.5.clone.1 | convolution fusion | flops 1086320640 | bytes 18628612 | tf_op jit(solution)/shard_map/while/body/eval_jaxpr/rkgd,ckd->kgrc/dot_general | solution.py:30
  130.9 4.0 %fusion.43 = f32[8,512]{1,0:T(8,128)S(1)} fusion(f32[1024,512,8]{1,0,2:T(8,128)S(1)} %get-tuple-element.334, f32[8,512]{1,0:T(8,128)S(1)} %get-tuple-element.332, pred[512,1024]{0,1:T(8,128)(4,1)S(1)} %compare_and_fusion.2), kind=kLoop, calls=%fused_computation.7.clone.1 | loop fusion | flops 20967424 | bytes 17334272 | tf_op jit(solution)/shard_map/while/body/eval_jaxpr/reduce_sum | solution.py:37
  135.0 6.1 %bitcast_add_fusion.2 = f32[1,8,512,128]{3,2,1,0:T(8,128)S(1)} fusion(f32[1,8,512,128]{3,2,1,0:T(8,128)S(1)} %copy-done.1, f32[1024,512,8]{1,0,2:T(8,128)S(1)} %get-tuple-element.334, f32[8,512]{1,0:T(8,128)S(1)} %get-tuple-element.332, pred[512,1024]{0,1:T(8,128)(4,1)S(1)} %compare_and_fusion.2, f32[8,512]{1,0:T(8,128)S(1)} %get-tuple-element.336, ...), kind=kOutput, calls=%fused_computation.11.clone.1 | convolution fusion | flops 1096810496 | bytes 21807108 | tf_op jit(solution)/shard_map/while/body/eval_jaxpr/kgrc,ckd->kgrd/dot_general | solution.py:38
  141.2 1.3 copy-done.2
  142.5 2.0 %fusion.26 = bf16[512,1,8,128]{3,0,2,1:T(8,128)(2,1)S(1)} fusion(f32[1,8,512,128]{3,2,1,0:T(8,128)} %get-tuple-element.175, f32[8,512]{1,0:T(8,128)S(1)} %bitcast.122), kind=kLoop, calls=%fused_computation.42 | loop fusion | flops 1048576 | bytes 3162112 | tf_op jit(solution)/shard_map/convert_element_type | solution.py:108
  144.4 0.7 copy.19
  145.6 30.0 %all_to_all.70 = bf16[8,64,1024]{2,1,0:T(8,128)(2,1)S(1)} all-to-all(bf16[8,64,1024]{2,1,0:T(8,128)(2,1)S(1)} %convert_element_type.19), channel_id=1, replica_groups=mesh['head'=8,'kv'=4] {'head'}, dimensions={0} | all-to-all | bytes 2097152 | tf_op jit(solution)/shard_map/all_to_all | solution.py:109
  175.6 1.1 copy.25
  (32 shorter events, 1.1 us)
Async XLA Ops:
  0.0 0.9 copy-start
  1.6 13.1 %all-to-all-start = ((bf16[64,8,128]{2,0,1:T(8,128)(2,1)}), bf16[64,8,128]{2,0,1:T(8,128)(2,1)S(1)}, u32[]{:S(2)}, u32[]{:S(2)}) async-start(bf16[64,8,128]{2,0,1:T(8,128)(2,1)} %copy_bitcast_fusion.2), calls=%async_computation | async-start | bytes 262144 | tf_op jit(solution)/shard_map/all_to_all | solution.py:69
  14.7 10.1 %all-to-all-start.2 = ((bf16[64,8,128]{2,0,1:T(8,128)(2,1)}), bf16[64,8,128]{2,0,1:T(8,128)(2,1)S(1)}, u32[]{:S(2)}, u32[]{:S(2)}) async-start(bf16[64,8,128]{2,0,1:T(8,128)(2,1)} %copy_bitcast_fusion.1), calls=%async_computation.2 | async-start | bytes 262144 | tf_op jit(solution)/shard_map/all_to_all | solution.py:70
  24.8 74.1 %all-to-all-start.1 = ((bf16[64,8,1024]{2,0,1:T(8,128)(2,1)}), bf16[64,8,1024]{2,0,1:T(8,128)(2,1)S(1)}, u32[]{:S(2)}, u32[]{:S(2)}) async-start(bf16[64,8,1024]{2,0,1:T(8,128)(2,1)} %bitcast.93), calls=%async_computation.1 | async-start | bytes 2097152 | tf_op jit(solution)/shard_map/all_to_all | solution.py:68
  109.3 4.1 %copy-start.1 = (f32[1,8,512,128]{3,2,1,0:T(8,128)S(1)}, f32[1,8,512,128]{3,2,1,0:T(8,128)}, u32[]{:S(2)}) copy-start(f32[1,8,512,128]{3,2,1,0:T(8,128)} %get-tuple-element.355) | copy-start | bytes 6291460 | tf_op jit(solution)/shard_map/while
  119.6 1.3 copy-start.2
  130.9 4.1 %copy-start.1 = (f32[1,8,512,128]{3,2,1,0:T(8,128)S(1)}, f32[1,8,512,128]{3,2,1,0:T(8,128)}, u32[]{:S(2)}) copy-start(f32[1,8,512,128]{3,2,1,0:T(8,128)} %get-tuple-element.355) | copy-start | bytes 6291460 | tf_op jit(solution)/shard_map/while
  141.1 1.3 copy-start.2
where the time goes:
time: 177 us
  blocking collectives  94.4 us (53%)
  local copies, waits for them, and re-layouts  28.4 us (16%)
  matrix products  18.1 us (10%)
  starting transfers between devices  13.3 us (8%)
  other arithmetic  11.8 us (7%)
  waiting for transfers between devices  9.58 us (5%)
    unnamed x1, blocking collectives  43.9 us
    all_to_all x1, blocking collectives, local(): lax.all_to_all(result, 'head', split_axis=0, concat_axis=1, tiled=True)  30 us
    gather x2, local copies, waits for them, and re-layouts, one_step(): key_doc = jnp.take(doc_global, key_pos)  12.3 us
    dot_general x2, matrix products, block_terms(): jnp.einsum('kgrc,ckd->kgrd', weights.astype(jnp.bfloat16), value_heads, p...  12.3 us
    all_gather x1, blocking collectives, local(): value_piece = lax.all_gather(value_block, 'kv', axis=0, tiled=True)  11.6 us
    all_gather x1, blocking collectives, local(): key_piece = lax.all_gather(key_block, 'kv', axis=0, tiled=True)  9 us
    reduce_sum x2, other arithmetic, block_terms(): row_total = jnp.sum(weights, axis=-1)  8.05 us
    all_to_all x1, starting transfers between devices, local(): lax.all_to_all(key_send, 'head', split_axis=1, concat_axis=0, tiled=True)  6.35 us
  transfers between devices with their start and end apart: 3, of which 2 were waited for; matrix products, arithmetic and copies ran while one was open for 5% of the time, Pallas kernels for 0%

commit v1 on v0

v1 whole, which is shorter than its diff:
```python
import functools
import math

import jax
import jax.numpy as jnp
from jax import lax
from jax.experimental import pallas as pl
from jax.experimental.pallas import tpu as pltpu
from jax.sharding import PartitionSpec as P

QUERY_HEADS = 64
KEY_VALUE_HEADS = 8
HEAD_SIZE = 128
CORES = 2
NEG_FILL = -1e30
SCALE_LOG2 = HEAD_SIZE ** -0.5 * math.log2(math.e)
MESH = pl.DeviceIdType.MESH


def peer_id(slot, level):
    return {"kv": slot // CORES, "head": level * CORES + slot % CORES}


def place():
    kv_here, head_here = lax.axis_index("kv"), lax.axis_index("head")
    return kv_here, head_here // CORES, lax.rem(head_here, CORES)


def gather_kernel(slots, levels, q_ref, k_ref, v_ref, d_ref, qo, ko, vo, do, sems):
    kv_here, level, core = place()
    me = kv_here * CORES + core
    width = q_ref.shape[1] // slots
    query_heads = width // HEAD_SIZE
    group = QUERY_HEADS // KEY_VALUE_HEADS
    slab_send, slab_recv, line_send, line_recv, own = sems

    barrier = pltpu.get_barrier_semaphore()
    for step in range(1, slots):
        peer = lax.rem(me + step, slots)
        pl.semaphore_signal(barrier, inc=1, device_id=peer_id(peer, level), device_id_type=MESH)

    @pl.when(level > 0)
    def _():
        pl.semaphore_signal(barrier, inc=1, device_id=peer_id(me, level - 1), device_id_type=MESH)

    @pl.when(level < levels - 1)
    def _():
        pl.semaphore_signal(barrier, inc=1, device_id=peer_id(me, level + 1), device_id_type=MESH)

    def parts(slot):
        kv_column = pl.multiple_of((slot * query_heads // group) * HEAD_SIZE, HEAD_SIZE)
        q_column = pl.multiple_of(slot * width, HEAD_SIZE)
        return (
            (k_ref.at[:, pl.ds(kv_column, HEAD_SIZE)], ko.at[kv_here, level, core]),
            (v_ref.at[:, pl.ds(kv_column, HEAD_SIZE)], vo.at[kv_here, level, core]),
            (d_ref, do.at[kv_here, level, core]),
            (q_ref.at[:, pl.ds(q_column, width)], qo.at[kv_here, core]),
        )

    local = [pltpu.make_async_copy(s, d, own.at[i]) for i, (s, d) in enumerate(parts(me))]
    for copy in local:
        copy.start()
    pl.semaphore_wait(
        barrier,
        slots - 1 + (level > 0).astype(jnp.int32) + (level < levels - 1).astype(jnp.int32),
    )

    def slab_copy(step, part):
        peer = lax.rem(me + step, slots)
        source, target = parts(peer)[part]
        return pltpu.make_async_remote_copy(
            src_ref=source, dst_ref=target,
            send_sem=slab_send.at[part, peer], recv_sem=slab_recv.at[part, me],
            device_id=peer_id(peer, level), device_id_type=MESH,
        )

    for part in range(4):
        for step in range(1, slots):
            slab_copy(step, part).start()

    def slab_wait(part, source):
        target = (
            ko.at[source // CORES, level, lax.rem(source, CORES)],
            vo.at[source // CORES, level, lax.rem(source, CORES)],
            do.at[source // CORES, level, lax.rem(source, CORES)],
            qo.at[source // CORES, lax.rem(source, CORES)],
        )[part]
        pltpu.make_async_remote_copy(
            src_ref=target, dst_ref=target,
            send_sem=slab_send.at[part, source], recv_sem=slab_recv.at[part, source],
            device_id=peer_id(source, level), device_id_type=MESH,
        ).wait_recv()

    buffers = (ko, vo, do)

    def line_copy(part, strip, slab, up):
        ref = buffers[part].at[strip, slab]
        return pltpu.make_async_remote_copy(
            src_ref=ref, dst_ref=ref,
            send_sem=line_send.at[part, strip, slab, 1 if up else 0],
            recv_sem=line_recv.at[part, strip, slab],
            device_id=peer_id(me, level + 1 if up else level - 1), device_id_type=MESH,
        )

    for copy in local:
        copy.wait()
    strips = slots // CORES

    def line_send_all(strip, slab, up, act):
        for part in range(3):
            copy = line_copy(part, strip, slab, up)
            copy.start() if act else copy.wait_send()

    for ahead in range(strips):
        strip = lax.rem(kv_here + ahead, strips)
        for source_core in range(CORES):
            source = strip * CORES + source_core

            @pl.when(source != me)
            def _():
                for part in range(3):
                    slab_wait(part, source)

        @pl.when(level < levels - 1)
        def _():
            line_send_all(strip, level, True, True)

        @pl.when(level > 0)
        def _():
            line_send_all(strip, level, False, True)

    for step in range(1, levels):
        for ahead in range(strips):
            strip = lax.rem(kv_here + ahead, strips)
            for up in (True, False):
                slab = level - step if up else level + step
                exists = (slab >= 0) if up else (slab < levels)
                onward = (level < levels - 1) if up else (level > 0)

                @pl.when(exists)
                def _():
                    for part in range(3):
                        line_copy(part, strip, slab, True).wait_recv()

                @pl.when(exists & onward)
                def _():
                    line_send_all(strip, slab, up, True)

    for step in range(0, levels):
        for strip in range(strips):
            for up in (True, False):
                slab = level - step if up else level + step
                exists = (slab >= 0) if up else (slab < levels)
                onward = (level < levels - 1) if up else (level > 0)

                @pl.when(exists & onward)
                def _():
                    line_send_all(strip, slab, up, False)

    for step in range(1, slots):
        slab_wait(3, lax.rem(me + step, slots))
    for part in range(4):
        for step in range(1, slots):
            slab_copy(step, part).wait_send()


def attend_kernel(levels, heads, tokens, span, docs_ref, q_ref, k_ref, v_ref, d_ref, o_ref, acc):
    strips = q_ref.shape[0]
    rows = CORES * tokens
    level = lax.axis_index("head") // CORES
    pairs = heads // 2
    chunk = span // rows
    blocks = k_ref.shape[0] // span

    def one_strip(strip, carry):
        own_chunk = strip * levels + level
        first_doc = docs_ref[own_chunk * CORES, 0]
        high = own_chunk // chunk + 1

        def count(block, low):
            last = docs_ref[(block + 1) * chunk * CORES - 1, rows - 1]
            return low + jnp.where(last < first_doc, 1, 0)

        low = lax.fori_loop(0, high - 1, count, 0)
        acc[...] = jnp.zeros_like(acc)
        own_docs = d_ref[own_chunk * CORES] + d_ref[own_chunk * CORES + 1]
        query_pos = own_chunk * rows + lax.broadcasted_iota(jnp.int32, (span, rows), 1)

        def one_block(block, state):
            first = pl.multiple_of(block * span, span)
            keys = k_ref[pl.ds(first, span), :]
            values = v_ref[pl.ds(first, span), :]
            key_docs = []
            for piece in range(chunk):
                at = (block * chunk + piece) * CORES
                key_docs.append(jnp.broadcast_to(d_ref[at] + d_ref[at + 1], (rows, rows)).T)
            key_docs = jnp.concatenate(key_docs, axis=0)
            key_pos = first + lax.broadcasted_iota(jnp.int32, (span, rows), 0)
            allowed = (key_docs == own_docs) & (key_pos <= query_pos)
            bias = jnp.where(allowed, 0.0, NEG_FILL)
            bias = jnp.concatenate([bias, bias], axis=1)
            peaks, totals = [], []
            for pair in range(pairs):
                queries = jnp.concatenate(
                    [
                        q_ref[strip, core, :, h * HEAD_SIZE:(h + 1) * HEAD_SIZE]
                        for h in (2 * pair, 2 * pair + 1)
                        for core in range(CORES)
                    ],
                    axis=0,
                )
                scores = lax.dot_general(
                    keys, queries, (((1,), (1,)), ((), ())), preferred_element_type=jnp.float32
                )
                scores = jnp.where(bias < 0.0, NEG_FILL, scores)
                peak = jnp.maximum(state[0][pair], jnp.max(scores, axis=0, keepdims=True))
                weights = jnp.exp2((scores - peak) * SCALE_LOG2)
                factor = jnp.exp2((state[0][pair] - peak) * SCALE_LOG2)
                peaks.append(peak)
                totals.append(
                    state[1][pair] * factor + jnp.sum(weights, axis=0, keepdims=True)
                )
                acc[pair] = acc[pair] * factor + lax.dot_general(
                    values, weights.astype(jnp.bfloat16), (((0,), (0,)), ((), ())),
                    preferred_element_type=jnp.float32,
                )
            return tuple(peaks), tuple(totals)

        start = (
            tuple(jnp.full((1, 2 * rows), NEG_FILL, jnp.float32) for _ in range(pairs)),
            tuple(jnp.zeros((1, 2 * rows), jnp.float32) for _ in range(pairs)),
        )
        _, totals = lax.fori_loop(low, high, one_block, start)
        for pair in range(pairs):
            result = acc[pair] / totals[pair]
            for half in range(2):
                head = 2 * pair + half
                turned = result[:, half * rows:(half + 1) * rows].T.astype(jnp.bfloat16)
                for core in range(CORES):
                    o_ref[strip, core, :, head * HEAD_SIZE:(head + 1) * HEAD_SIZE] = turned[
                        core * tokens:(core + 1) * tokens
                    ]
        return carry

    lax.fori_loop(0, strips, one_strip, 0)


def return_kernel(slots, a_ref, o_ref, send, recv, own):
    kv_here, level, core = place()
    me = kv_here * CORES + core
    width = a_ref.shape[3]
    barrier = pltpu.get_barrier_semaphore()
    for step in range(1, slots):
        peer = lax.rem(me + step, slots)
        pl.semaphore_signal(barrier, inc=1, device_id=peer_id(peer, level), device_id_type=MESH)

    def target(slot):
        return o_ref.at[:, pl.ds(pl.multiple_of(slot * width, HEAD_SIZE), width)]

    local = pltpu.make_async_copy(a_ref.at[kv_here, core], target(me), own)
    local.start()
    pl.semaphore_wait(barrier, slots - 1)

    def copy(step):
        peer = lax.rem(me + step, slots)
        return pltpu.make_async_remote_copy(
            src_ref=a_ref.at[peer // CORES, lax.rem(peer, CORES)], dst_ref=target(me),
            send_sem=send.at[peer], recv_sem=recv.at[me],
            device_id=peer_id(peer, level), device_id_type=MESH,
        )

    for step in range(1, slots):
        copy(step).start()
    for step in range(1, slots):
        source = lax.rem(me + step, slots)
        pltpu.make_async_remote_copy(
            src_ref=target(source), dst_ref=target(source),
            send_sem=send.at[source], recv_sem=recv.at[source],
            device_id=peer_id(source, level), device_id_type=MESH,
        ).wait_recv()
    for step in range(1, slots):
        copy(step).wait_send()
    local.wait()


def local(strips, levels, queries, key_rows, value_matrix, doc_ids):
    slots = strips * CORES
    tokens, columns = queries.shape
    width = columns // slots
    heads = width // HEAD_SIZE
    sequence = tokens * slots * levels
    core = lax.rem(lax.axis_index("head"), CORES)
    doc_row = jnp.stack([doc_ids, doc_ids])
    doc_row = jnp.where(jnp.arange(CORES)[:, None] == core, doc_row, 0)
    doc_row = doc_row.reshape(1, CORES * tokens)
    vmem = pl.BlockSpec(memory_space=pltpu.VMEM)
    anywhere = pl.BlockSpec(memory_space=pl.ANY)
    bf16 = jnp.bfloat16
    dma = pltpu.SemaphoreType.DMA
    query_block, key_block, value_block, docs = pl.pallas_call(
        functools.partial(gather_kernel, slots, levels),
        name="gather",
        out_shape=(
            jax.ShapeDtypeStruct((strips, CORES, tokens, width), bf16),
            jax.ShapeDtypeStruct((strips, levels, CORES, tokens, HEAD_SIZE), bf16),
            jax.ShapeDtypeStruct((strips, levels, CORES, tokens, HEAD_SIZE), bf16),
            jax.ShapeDtypeStruct((strips, levels, CORES, 1, CORES * tokens), jnp.int32),
        ),
        in_specs=[anywhere, anywhere, anywhere, vmem],
        out_specs=(vmem, vmem, vmem, vmem),
        scratch_shapes=[(
            dma((4, slots)), dma((4, slots)),
            dma((3, strips, levels, 2)), dma((3, strips, levels)), dma((4,)),
        )],
        compiler_params=pltpu.CompilerParams(collective_id=0, has_side_effects=True),
    )(queries, key_rows, value_matrix, doc_row)
    docs = docs.reshape(sequence // tokens, 1, CORES * tokens)
    span = 2 * CORES * tokens
    attended = pl.pallas_call(
        functools.partial(attend_kernel, levels, heads, tokens, span),
        name="attend",
        out_shape=jax.ShapeDtypeStruct((strips, CORES, tokens, width), bf16),
        in_specs=[pl.BlockSpec(memory_space=pltpu.SMEM), vmem, vmem, vmem, vmem],
        out_specs=vmem,
        scratch_shapes=[
            pltpu.VMEM((heads // 2, HEAD_SIZE, 2 * CORES * tokens), jnp.float32),
        ],
    )(
        docs.reshape(sequence // tokens, CORES * tokens),
        query_block,
        key_block.reshape(sequence, HEAD_SIZE),
        value_block.reshape(sequence, HEAD_SIZE),
        docs,
    )
    return pl.pallas_call(
        functools.partial(return_kernel, slots),
        name="give_back",
        out_shape=jax.ShapeDtypeStruct((tokens, columns), bf16),
        in_specs=[vmem],
        out_specs=anywhere,
        scratch_shapes=[dma((slots,)), dma((slots,)), dma],
        compiler_params=pltpu.CompilerParams(collective_id=1, has_side_effects=True),
    )(attended)


def solution(mesh):
    rows = P(("kv", "head"), None)
    return jax.shard_map(
        functools.partial(local, mesh.shape["kv"], mesh.shape["head"] // CORES),
        mesh=mesh,
        in_specs=(rows, rows, rows, P(("kv", "head"))),
        out_specs=rows,
        check_vma=False,
    )
```

time: 177 us -> 70.7 us (0.40)
  the two profiles are of different devices: /device:TPU:0 before, /device:TPU:17 now
where the time goes in v1:
time: 70.7 us; the launch traced here: 70.6 us
  Pallas kernels  67 us (95%)
  local copies, waits for them, and re-layouts  3.51 us (5%)
    pallas_call x1, Pallas kernels, local(): pl.pallas_call(functools.partial(gather_kernel, slots, levels), name='gat...  30.6 us
    pallas_call x1, Pallas kernels, local(): pl.pallas_call(functools.partial(attend_kernel, levels, heads, tokens, sp...  19.1 us
    pallas_call x1, Pallas kernels, local(): pl.pallas_call(functools.partial(return_kernel, slots), name='give_back',...  17.3 us
    unnamed x3, local copies, waits for them, and re-layouts  2.91 us

profile of v1, /device:TPU:17, one launch (start us, length us, event | category | flops | bytes accessed | tf_op | source)
XLA Modules:
  0.0 70.6 jit_solution(14805408737612441846)
XLA Ops:
  0.0 0.0 copy-start
  0.0 0.6 copy-done
  0.7 0.1 add_select_fusion
  0.7 0.6 select_n.15.d_ref
  1.3 30.6 %gather.1 = (bf16[4,2,64,1024]{3,2,1,0:T(8,128)(2,1)}, bf16[4,4,2,64,128]{4,3,2,1,0:T(8,128)(2,1)}, bf16[4,4,2,64,128]{4,3,2,1,0:T(8,128)(2,1)}, s32[4,4,2,1,128]{4,3,2,1,0:T(1,128)}) custom-call(bf16[64,8192]{1,0:T(8,128)(2,1)} %q_ref.1, bf16[64,1024]{1,0:T(8,128)(2,1)} %k_ref.1, bf16[64,1024]{1,0:T(8,128)(2,1)} %v_ref.1, s32[1,128]{1,0:T(1,128)} %select_n.15.d_ref), custom_call_target="tpu_custom_call" | custom-call | tf_op jit(solution)/shard_map/gather/pallas_call | solution.py:300
  31.9 19.1 %attend.1.a_ref = bf16[4,2,64,1024]{3,2,1,0:T(8,128)(2,1)} custom-call(s32[32,128]{1,0:T(8,128)} %bitcast.7, bf16[4,2,64,1024]{3,2,1,0:T(8,128)(2,1)} %get-tuple-element.10.q_ref, bf16[2048,128]{1,0:T(8,128)(2,1)} %bitcast.5, bf16[2048,128]{1,0:T(8,128)(2,1)} %bitcast.6, s32[32,1,128]{2,1,0:T(1,128)} %bitcast.8), custom_call_target="tpu_custom_call" | custom-call | tf_op jit(solution)/shard_map/attend/pallas_call | solution.py:319
  51.1 17.3 %give_back.1 = bf16[64,8192]{1,0:T(8,128)(2,1)} custom-call(bf16[4,2,64,1024]{3,2,1,0:T(8,128)(2,1)} %attend.1.a_ref), custom_call_target="tpu_custom_call" | custom-call | tf_op jit(solution)/shard_map/give_back/pallas_call | solution.py:335
  68.3 2.3 %copy.6 = bf16[64,8192]{1,0:T(8,128)(2,1)} copy(bf16[64,8192]{1,0:T(8,128)(2,1)} %give_back.1) | data formatting | bytes 2097152
  (1 shorter events, 0.0 us)
Async XLA Ops:
  0.0 0.7 copy-start
